TPU v7x, 32 devices: a whole 2x2x4 slice. The times are simulated.
32 devices in a mesh: ga: 2 (over x), ta: 4 (over y, core), gy: 4 (over z).
Axes of the slice: x: 2, y: 2, z: 4, core: 2. Of those that a mesh axis runs over, the one named last changes fastest.
Arguments:
- clip: bfloat16 [32, 16, 64, 512], P(('ga', 'ta'), 'gy'), parts along dimension 0, may hold values from -6 to 6
- w_space: bfloat16 [3, 3, 512, 512], replicated, may hold values from -0.09375 to 0.09375
- w_time: bfloat16 [3, 512, 512], replicated, may hold values from -0.15625 to 0.15625
- w_qkv: bfloat16 [512, 1536], replicated, may hold values from -0.61871843 to 0.61871843
- w_out: bfloat16 [512, 512], replicated, may hold values from -0.25 to 0.25
- norm_gain: float32 [512], replicated, may hold values from 0.1 to 1.9
Outputs:
- block_out: bfloat16 [32, 16, 64, 512], P(('ga', 'ta'), 'gy'), parts along dimension 0
There are 2 independent parts, one for each index of `ga`. A program takes and returns all parts, laid end to end along the dimension named above; an argument that names none is the same for every part. Nothing has to cross between parts.
All inputs are finite; a program needn't handle non-finite values.
Results may differ from a plain program's by a relative error of at most 0.0085.
Values may be sent and summed in bfloat16 or wider, within the bound.
No kernel may reach another device: no remote copies, remote signals or barrier semaphores. Data moves between devices by JAX's collectives and lax.ppermute only.
A program may use at most 64 MiB of HBM per device.

v0:
```python
import jax
import jax.numpy as jnp
from jax import lax
from jax.sharding import PartitionSpec as P

HEADS = 8


def padded_2(block, sides, width):
    for axis, dim in sides:
        count = lax.axis_size(axis)
        forward = [(i, i + 1) for i in range(count - 1)]
        backward = [(target, source) for source, target in forward]
        low = lax.ppermute(
            lax.slice_in_dim(block, block.shape[dim] - width, None, axis=dim), axis, forward
        )
        high = lax.ppermute(lax.slice_in_dim(block, 0, width, axis=dim), axis, backward)
        block = jnp.concatenate([low, block, high], axis=dim)
    return block


def from_behind(array, axis, by):
    devices = lax.axis_size(axis)
    pairs = [(i, i + by) for i in range(devices) if 0 <= i + by < devices]
    return lax.ppermute(array, axis, pairs)


def conv_space(padded, w_space, height, width):
    channels = padded.shape[-1]
    total = jnp.zeros(padded.shape[:1] + (height, width, channels), jnp.float32)
    for row_off in range(3):
        for col_off in range(3):
            window = padded[:, row_off : row_off + height, col_off : col_off + width, :]
            product = jnp.dot(
                window.reshape(-1, channels),
                w_space[row_off, col_off],
                preferred_element_type=jnp.float32,
            )
            total = total + product.reshape(total.shape)
    return total


def temporal_mix(clip, hidden, earlier, w_time, norm_gain):
    channels = clip.shape[-1]
    frames = hidden.shape[0]
    joined = jnp.concatenate([earlier, hidden], axis=0)
    total = jnp.zeros(hidden.shape, jnp.float32)
    for tap_index in range(3):
        window = joined[2 - tap_index : 2 - tap_index + frames]
        product = jnp.dot(
            window.reshape(-1, channels), w_time[tap_index], preferred_element_type=jnp.float32
        )
        total = total + product.reshape(hidden.shape)
    mixed = (clip.astype(jnp.float32) + total).astype(jnp.bfloat16)
    wide = mixed.astype(jnp.float32)
    scale = lax.rsqrt(jnp.mean(wide * wide, axis=-1, keepdims=True) + 1e-06)
    normed = (wide * scale * norm_gain).astype(jnp.bfloat16)
    return (mixed, normed)


def project(normed, w_qkv):
    channels = normed.shape[-1]
    flattened = jnp.dot(
        normed.reshape(-1, channels), w_qkv, preferred_element_type=jnp.float32
    ).astype(jnp.bfloat16)
    joined = flattened.reshape(normed.shape[:-1] + (3 * channels,))
    return (
        joined[..., :channels],
        joined[..., channels : 2 * channels],
        joined[..., 2 * channels :],
    )


def attend(queries, keyset, valueset, heads):
    frames, rows, cols, channels = queries.shape
    head_dim = channels // heads
    shape = (frames, rows, cols, heads, head_dim)
    scores = jnp.einsum(
        "frwhd,grwhd->rwhfg",
        queries.reshape(shape),
        keyset.reshape(shape),
        preferred_element_type=jnp.float32,
    )
    scores = scores * (1.0 / head_dim**0.5)
    peak = jnp.max(scores, axis=-1, keepdims=True)
    expo = jnp.exp(scores - peak)
    probs = (expo / jnp.sum(expo, axis=-1, keepdims=True)).astype(jnp.bfloat16)
    output = jnp.einsum(
        "rwhfg,grwhd->frwhd", probs, valueset.reshape(shape), preferred_element_type=jnp.float32
    )
    return output.reshape(queries.shape).astype(jnp.bfloat16)


def attend_back(queries, keyset, valueset):
    output = attend(queries, keyset, valueset, HEADS)
    return lax.all_to_all(output, "ta", split_axis=0, concat_axis=2, tiled=True)


def per_device(clip, w_space, w_time, w_qkv, w_out, norm_gain):
    frames, height, width, channels = clip.shape
    rimmed = padded_2(clip, (("gy", 1),), 1)
    padded = jnp.pad(rimmed, ((0, 0), (0, 0), (1, 1), (0, 0)))
    hidden = jax.nn.silu(conv_space(padded, w_space, height, width)).astype(jnp.bfloat16)
    earlier = from_behind(hidden[-2:], "ta", 1)
    mixed, normed = temporal_mix(clip, hidden, earlier, w_time, norm_gain)
    queries, keyset, valueset = project(
        lax.all_to_all(normed, "ta", split_axis=2, concat_axis=0, tiled=True), w_qkv
    )
    attended = attend_back(queries, keyset, valueset)
    projected = jnp.dot(
        attended.reshape(-1, channels), w_out, preferred_element_type=jnp.float32
    ).reshape(clip.shape)
    return (mixed.astype(jnp.float32) + projected).astype(jnp.bfloat16)


def solution(mesh):
    in_specs = (P(("ga", "ta"), "gy", None, None), P(), P(), P(), P(), P())
    out_specs = P(("ga", "ta"), "gy", None, None)
    return jax.shard_map(
        per_device, mesh=mesh, in_specs=in_specs, out_specs=out_specs, check_vma=False
    )
```

profile of v0, /device:TPU:0, one launch (start us, length us, event | category | flops | bytes accessed | tf_op | source)
XLA Modules:
  0.0 112.8 jit_solution(17687621035857392692)
XLA Ops:
  0.0 0.0 copy-start
  0.0 1.2 %fusion.79 = (bf16[4,1,64,512]{3,2,1,0:T(8,128)(2,1)S(1)}, bf16[4,1,64,512]{3,2,1,0:T(8,128)(2,1)S(1)}) fusion(bf16[4,4,64,512]{3,2,1,0:T(8,128)(2,1)} %param.6), kind=kLoop, calls=%fused_computation.87 | loop fusion | bytes 1048576 | tf_op jit(solution)/shard_map/slice | solution.py:15
  1.2 5.0 %collective-permute-start = (bf16[4,1,64,512]{3,2,1,0:T(8,128)(2,1)S(1)}, bf16[4,1,64,512]{3,2,1,0:T(8,128)(2,1)S(1)}, u32[]{:S(2)}, u32[]{:S(2)}) collective-permute-start(bf16[4,1,64,512]{3,2,1,0:T(8,128)(2,1)S(1)} %get-tuple-element.8), channel_id=1, source_target_pairs={{0,1},{1,2},{2,3},{4,5},{5,6},{6,7},{8,9},{9,10},{10,11},{12,13},{... | collective-permute-start | bytes 786440 | tf_op jit(solution)/shard_map/ppermute | solution.py:14
  6.2 0.0 copy-start.2
  6.2 1.4 %collective-permute-start.1 = (bf16[4,1,64,512]{3,2,1,0:T(8,128)(2,1)S(1)}, bf16[4,1,64,512]{3,2,1,0:T(8,128)(2,1)S(1)}, u32[]{:S(2)}, u32[]{:S(2)}) collective-permute-start(bf16[4,1,64,512]{3,2,1,0:T(8,128)(2,1)S(1)} %get-tuple-element.9), channel_id=1, source_target_pairs={{1,0},{2,1},{3,2},{5,4},{6,5},{7,6},{9,8},{10,9},{11,10},{13,12},{... | collective-permute-start | bytes 786440 | tf_op jit(solution)/shard_map/ppermute | solution.py:17
  7.6 0.0 copy-start.4
  7.6 2.2 %fusion.55 = f32[4,4,64,512]{3,2,1,0:T(8,128)S(1)} fusion(bf16[4,4,64,512]{3,2,1,0:T(8,128)(2,1)} %param.6, bf16[3,3,512,512]{3,2,1,0:T(8,128)(2,1)} %param.7), kind=kOutput, calls=%fused_computation.62 | convolution fusion | flops 536870912 | bytes 3670016 | tf_op jit(solution)/shard_map/dot_general | solution.py:34
  9.8 1.9 %collective-permute-done = bf16[4,1,64,512]{3,2,1,0:T(8,128)(2,1)S(1)} collective-permute-done((bf16[4,1,64,512]{3,2,1,0:T(8,128)(2,1)S(1)}, bf16[4,1,64,512]{3,2,1,0:T(8,128)(2,1)S(1)}, u32[]{:S(2)}, u32[]{:S(2)}) %collective-permute-start) | collective-permute-done | bytes 262176 | tf_op jit(solution)/shard_map/ppermute | solution.py:14
  11.7 4.3 %collective-permute-done.1 = bf16[4,1,64,512]{3,2,1,0:T(8,128)(2,1)S(1)} collective-permute-done((bf16[4,1,64,512]{3,2,1,0:T(8,128)(2,1)S(1)}, bf16[4,1,64,512]{3,2,1,0:T(8,128)(2,1)S(1)}, u32[]{:S(2)}, u32[]{:S(2)}) %collective-permute-start.1) | collective-permute-done | bytes 262176 | tf_op jit(solution)/shard_map/ppermute | solution.py:17
  16.0 0.0 copy-done.2
  16.0 0.9 fusion.22
  16.9 0.0 copy-done.4
  16.9 0.7 fusion.35
  17.6 0.7 fusion.37
  18.3 0.7 fusion.39
  19.0 0.7 fusion.41
  19.8 0.7 fusion.43
  20.5 0.7 fusion.23
  21.2 0.7 fusion.27
  21.9 0.0 copy-start.5
  21.9 1.4 %multiply_convert_fusion = bf16[4,4,64,512]{3,2,1,0:T(8,128)(2,1)S(1)} fusion(f32[4,4,64,512]{3,2,1,0:T(8,128)S(1)} %fusion.27, f32[4,4,64,512]{3,2,1,0:T(8,128)S(1)} %fusion.35, f32[4,4,64,512]{3,2,1,0:T(8,128)S(1)} %fusion.37, f32[4,4,64,512]{3,2,1,0:T(8,128)S(1)} %fusion.55, f32[4,4,64,512]{3,2,1,0:T(8,128)S(1)} %fusion.39, ...), kind=kOutput, calls=%fused_computation.25 | convolution fusion | flops 543686656 | bytes 19398656 | tf_op jit(solution)/shard_map/dot_general | solution.py:34
  23.4 1.3 %collective-permute-start.2 = (bf16[2,4,64,512]{3,2,1,0:T(8,128)(2,1)S(1)}, bf16[2,4,64,512]{3,2,1,0:T(8,128)(2,1)S(1)}, u32[]{:S(2)}, u32[]{:S(2)}) collective-permute-start(bf16[2,4,64,512]{3,2,1,0:T(8,128)(2,1)S(1)} %slice.124), channel_id=1, source_target_pairs={{0,4},{4,8},{8,12},{1,5},{5,9},{9,13},{2,6},{6,10},{10,14},{3,7},{... | collective-permute-start | bytes 1572872 | tf_op jit(solution)/shard_map/ppermute | solution.py:25
  24.7 0.0 copy-done.5
  24.7 0.7 fusion.49
  25.4 0.8 collective-permute-done.2
  26.2 0.7 fusion.45
  26.9 0.0 copy-start.6
  26.9 1.0 fusion.5
  27.9 0.0 copy-done.6
  28.0 0.3 fusion.7
  28.3 0.8 copy.22
  29.1 24.7 %all_to_all.30 = bf16[4,4,64,512]{3,1,0,2:T(4,128)(2,1)S(1)} all-to-all(bf16[4,4,64,512]{3,1,0,2:T(4,128)(2,1)S(1)} %copy.22), channel_id=1, replica_groups=mesh['ga'=2,'ta'=4,'gy'=4] {'ta'}, dimensions={2} | all-to-all | bytes 2097152 | tf_op jit(solution)/shard_map/all_to_all | solution.py:107
  53.8 0.6 copy.23
  54.4 0.1 copy.24
  54.5 1.8 %convolution_convert_fusion = bf16[1024,1536]{1,0:T(8,128)(2,1)S(1)} fusion(bf16[1024,512]{1,0:T(8,128)(2,1)S(1)} %bitcast.119, bf16[512,1536]{1,0:T(8,128)(2,1)S(1)} %copy-done), kind=kOutput, calls=%fused_computation.5 | convolution fusion | flops 1612185600 | bytes 5767168 | tf_op jit(solution)/shard_map/dot_general | solution.py:63
  56.3 1.7 %fusion.78 = (bf16[16,4,16,512]{3,2,1,0:T(8,128)(2,1)S(1)}, bf16[16,4,16,512]{3,2,1,0:T(8,128)(2,1)}, bf16[16,4,16,512]{3,2,1,0:T(8,128)(2,1)}) fusion(bf16[16,4,16,1536]{3,2,1,0:T(8,128)(2,1)S(1)} %bitcast.117), kind=kLoop, calls=%fused_computation.86 | loop fusion | bytes 6291456 | tf_op jit(solution)/shard_map/slice | solution.py:70
  57.9 2.1 %reshape.84 = bf16[16,4,16,8,64]{4,3,2,1,0:T(8,128)(2,1)} reshape(bf16[16,4,16,512]{3,2,1,0:T(8,128)(2,1)S(1)} %get-tuple-element.5) | data formatting | bytes 2097152 | tf_op jit(solution)/shard_map/reshape | solution.py:89
  60.0 2.8 %reshape.86 = bf16[16,4,16,8,64]{4,3,2,1,0:T(8,128)(2,1)S(1)} reshape(bf16[16,4,16,512]{3,2,1,0:T(8,128)(2,1)} %get-tuple-element.6) | data formatting | bytes 2097152 | tf_op jit(solution)/shard_map/reshape | solution.py:81
  62.8 3.9 %reshape.85 = bf16[16,4,16,8,64]{4,3,2,1,0:T(8,128)(2,1)} reshape(bf16[16,4,16,512]{3,2,1,0:T(8,128)(2,1)} %get-tuple-element.7) | data formatting | bytes 2097152 | tf_op jit(solution)/shard_map/reshape | solution.py:80
  66.7 4.1 %fusion.11 = f32[4,16,8,16,16]{3,4,2,1,0:T(8,128)S(1)} fusion(bf16[16,4,16,8,64]{4,3,2,1,0:T(8,128)(2,1)S(1)} %reshape.86, bf16[16,4,16,8,64]{4,3,2,1,0:T(8,128)(2,1)} %reshape.85), kind=kOutput, calls=%fused_computation.18 | convolution fusion | flops 16777216 | bytes 2621440 | tf_op jit(solution)/shard_map/frwhd,grwhd->rwhfg/dot_general | solution.py:78
  70.8 17.7 %fusion.80 = (f32[4,16,8,16]{3,2,1,0:T(8,128)S(1)}, f32[4,16,8,16,16]{3,4,2,1,0:T(8,128)S(1)}) fusion(f32[4,16,8,16,16]{3,4,2,1,0:T(8,128)S(1)} %fusion.11), kind=kOutput, calls=%fused_computation.88 | output fusion | flops 524303 | bytes 1081344 | tf_op jit(solution)/shard_map/sub | solution.py:86
  88.6 1.7 %convert_bitcast_fusion = bf16[16,4,16,8,64]{4,0,3,2,1:T(8,128)(2,1)S(1)} fusion(f32[4,16,8,16,16]{3,4,2,1,0:T(8,128)S(1)} %get-tuple-element.13, f32[4,16,8,16]{3,2,1,0:T(8,128)S(1)} %get-tuple-element.12, bf16[16,4,16,8,64]{4,3,2,1,0:T(8,128)(2,1)S(1)} %copy-done.3), kind=kOutput, calls=%fused_computation.21 | convolution fusion | flops 17563648 | bytes 2654208 | tf_op jit(solution)/shard_map/rwhfg,grwhd->frwhd/dot_general | solution.py:88
  90.3 0.5 copy.29
  90.9 2.0 %convert_element_type.45 = bf16[16,4,16,512]{3,2,1,0:T(8,128)(2,1)} reshape(bf16[16,4,16,8,64]{4,3,2,1,0:T(8,128)(2,1)S(1)} %copy.29) | data formatting | bytes 2097152 | tf_op jit(solution)/shard_map/convert_element_type | solution.py:91
  92.9 18.0 %all_to_all.31 = bf16[16,4,16,512]{3,2,1,0:T(8,128)(2,1)S(1)} all-to-all(bf16[16,4,16,512]{3,2,1,0:T(8,128)(2,1)} %convert_element_type.45), channel_id=1, replica_groups=mesh['ga'=2,'ta'=4,'gy'=4] {'ta'}, dimensions={0} | all-to-all | bytes 2097152 | tf_op jit(solution)/shard_map/all_to_all | solution.py:96
  111.0 0.1 copy.30
  111.1 0.0 copy-start.1
  111.1 1.7 %fusion.8 = bf16[4,4,64,512]{3,2,1,0:T(8,128)(2,1)} fusion(bf16[4,4,64,512]{3,2,1,0:T(8,128)(2,1)S(1)} %get-tuple-element.11, bf16[4,4,64,512]{3,2,1,0:T(8,128)(2,1)S(1)} %bitcast.118, bf16[512,512]{1,0:T(8,128)(2,1)S(1)} %copy-done.7), kind=kOutput, calls=%fused_computation.15 | convolution fusion | flops 538443776 | bytes 3670016 | tf_op jit(solution)/shard_map/dot_general | solution.py:110
  (8 shorter events, 0.1 us)
Async XLA Ops:
  0.0 54.4 %copy-start = (bf16[512,1536]{1,0:T(8,128)(2,1)S(1)}, bf16[512,1536]{1,0:T(8,128)(2,1)}, u32[]{:S(2)}) copy-start(bf16[512,1536]{1,0:T(8,128)(2,1)} %param.9) | copy-start | bytes 4718596
  1.2 10.5 %collective-permute-start = (bf16[4,1,64,512]{3,2,1,0:T(8,128)(2,1)S(1)}, bf16[4,1,64,512]{3,2,1,0:T(8,128)(2,1)S(1)}, u32[]{:S(2)}, u32[]{:S(2)}) collective-permute-start(bf16[4,1,64,512]{3,2,1,0:T(8,128)(2,1)S(1)} %get-tuple-element.8), channel_id=1, source_target_pairs={{0,1},{1,2},{2,3},{4,5},{5,6},{6,7},{8,9},{9,10},{10,11},{12,13},{... | collective-permute-start | bytes 786440 | tf_op jit(solution)/shard_map/ppermute | solution.py:14
  6.2 9.8 %copy-start.2 = (bf16[4,4,64,512]{3,2,1,0:T(8,128)(2,1)S(1)}, bf16[4,4,64,512]{3,2,1,0:T(8,128)(2,1)}, u32[]{:S(2)}) copy-start(bf16[4,4,64,512]{3,2,1,0:T(8,128)(2,1)} %param.6) | copy-start | bytes 3145732
  6.2 9.8 %collective-permute-start.1 = (bf16[4,1,64,512]{3,2,1,0:T(8,128)(2,1)S(1)}, bf16[4,1,64,512]{3,2,1,0:T(8,128)(2,1)S(1)}, u32[]{:S(2)}, u32[]{:S(2)}) collective-permute-start(bf16[4,1,64,512]{3,2,1,0:T(8,128)(2,1)S(1)} %get-tuple-element.9), channel_id=1, source_target_pairs={{1,0},{2,1},{3,2},{5,4},{6,5},{7,6},{9,8},{10,9},{11,10},{13,12},{... | collective-permute-start | bytes 786440 | tf_op jit(solution)/shard_map/ppermute | solution.py:17
  7.6 9.3 %copy-start.4 = (bf16[3,3,512,512]{3,2,1,0:T(8,128)(2,1)S(1)}, bf16[3,3,512,512]{3,2,1,0:T(8,128)(2,1)}, u32[]{:S(2)}) copy-start(bf16[3,3,512,512]{3,2,1,0:T(8,128)(2,1)} %param.7) | copy-start | bytes 14155780
  21.9 2.8 %copy-start.5 = (bf16[3,512,512]{2,1,0:T(8,128)(2,1)S(1)}, bf16[3,512,512]{2,1,0:T(8,128)(2,1)}, u32[]{:S(2)}) copy-start(bf16[3,512,512]{2,1,0:T(8,128)(2,1)} %param.8) | copy-start | bytes 4718596
  23.4 2.8 %collective-permute-start.2 = (bf16[2,4,64,512]{3,2,1,0:T(8,128)(2,1)S(1)}, bf16[2,4,64,512]{3,2,1,0:T(8,128)(2,1)S(1)}, u32[]{:S(2)}, u32[]{:S(2)}) collective-permute-start(bf16[2,4,64,512]{3,2,1,0:T(8,128)(2,1)S(1)} %slice.124), channel_id=1, source_target_pairs={{0,4},{4,8},{8,12},{1,5},{5,9},{9,13},{2,6},{6,10},{10,14},{3,7},{... | collective-permute-start | bytes 1572872 | tf_op jit(solution)/shard_map/ppermute | solution.py:25
  26.9 1.0 copy-start.6
  70.8 17.7 %copy-start.3 = (bf16[16,4,16,8,64]{4,3,2,1,0:T(8,128)(2,1)S(1)}, bf16[16,4,16,8,64]{4,3,2,1,0:T(8,128)(2,1)}, u32[]{:S(2)}) copy-start(bf16[16,4,16,8,64]{4,3,2,1,0:T(8,128)(2,1)} %reshape.84) | copy-start | bytes 3145732
  92.9 18.2 %copy-start.7 = (bf16[512,512]{1,0:T(8,128)(2,1)S(1)}, bf16[512,512]{1,0:T(8,128)(2,1)}, u32[]{:S(2)}) copy-start(bf16[512,512]{1,0:T(8,128)(2,1)} %param.10) | copy-start | bytes 1572868
  111.1 1.7 %copy-start.1 = (bf16[512,1536]{1,0:T(8,128)(2,1)S(1)}, bf16[512,1536]{1,0:T(8,128)(2,1)}, u32[]{:S(2)}) copy-start(bf16[512,1536]{1,0:T(8,128)(2,1)} %param.9) | copy-start | bytes 4718596
where the time goes:
time: 113 us
  blocking collectives  42.7 us (38%)
  matrix products  20.3 us (18%)
  other arithmetic  19 us (17%)
  local copies, waits for them, and re-layouts  15.9 us (14%)
  starting transfers between devices  7.72 us (7%)
  waiting for transfers between devices  6.9 us (6%)
    all_to_all x1, blocking collectives, per_device(): lax.all_to_all(normed, 'ta', split_axis=2, concat_axis=0, tiled=True)  24.7 us
    all_to_all x1, blocking collectives, attend_back(): return lax.all_to_all(output, 'ta', split_axis=0, concat_axis=2, tiled=True)  18 us
    sub x1, other arithmetic, attend(): expo = jnp.exp(scores - peak)  17.7 us
    dot_general x9, matrix products, conv_space(): jnp.dot(window.reshape(-1, channels), w_space[row_off, col_off], preferre...  8.59 us
    ppermute x1, starting transfers between devices, padded_2(): lax.ppermute(lax.slice_in_dim(block, block.shape[dim] - width, None, axis...  4.97 us
    ppermute x1, waiting for transfers between devices, padded_2(): lax.ppermute(lax.slice_in_dim(block, 0, width, axis=dim), axis, backward)  4.27 us
    dot_general x1, matrix products, attend(): jnp.einsum('frwhd,grwhd->rwhfg', queries.reshape(shape), keyset.reshape(s...  4.11 us
    reshape x1, local copies, waits for them, and re-layouts, attend(): queries.reshape(shape)  3.9 us
  transfers between devices with their start and end apart: 3, of which 3 were waited for; matrix products, arithmetic and copies ran while one was open for 3% of the time, Pallas kernels for 0%

commit v1 on v0

--- a/solution.py
+++ b/solution.py
@@ -1,9 +1,37 @@
+import functools
 import jax
 import jax.numpy as jnp
 from jax import lax
 from jax.sharding import PartitionSpec as P
 
 HEADS = 8
+
+
+def proceed_lines(own_rows, array_axis, row_data):
+    far_arr, now = (own_rows.shape[:array_axis], own_rows.shape[array_axis + 1 :])
+    return jnp.moveaxis(own_rows.reshape(*far_arr, row_data, -1, *now), array_axis, 0)
+
+
+def _solve_sums_all(base_x, dim_i):
+    base_x = jnp.moveaxis(base_x, 0, dim_i)
+    even = base_x.shape
+    return base_x.reshape(*even[:dim_i], even[dim_i] * even[dim_i + 1], *even[dim_i + 2 :])
+
+
+def try_all_the_sizes(a0, lane_axis, packet, local_x):
+    opened, answer = (lax.axis_size(lane_axis), lax.axis_index(lane_axis))
+    reply = proceed_lines(a0, packet, opened)
+    windows = [reply[answer]]
+    for hop_no in range(1, opened):
+        aux = reply[(answer + hop_no) % opened]
+        windows.append(
+            lax.ppermute(aux, lane_axis, [(kk, (kk + hop_no) % opened) for kk in range(opened)])
+        )
+    reply = jnp.stack(windows)[(answer - jnp.arange(opened)) % opened]
+    return _solve_sums_all(reply, local_x)
+
+
+begin_chains_all = functools.partial(try_all_the_sizes, lane_axis="ta", packet=2, local_x=0)
 
 
 def padded_2(block, sides, width):
@@ -103,9 +131,7 @@
     hidden = jax.nn.silu(conv_space(padded, w_space, height, width)).astype(jnp.bfloat16)
     earlier = from_behind(hidden[-2:], "ta", 1)
     mixed, normed = temporal_mix(clip, hidden, earlier, w_time, norm_gain)
-    queries, keyset, valueset = project(
-        lax.all_to_all(normed, "ta", split_axis=2, concat_axis=0, tiled=True), w_qkv
-    )
+    queries, keyset, valueset = project(begin_chains_all(normed), w_qkv)
     attended = attend_back(queries, keyset, valueset)
     projected = jnp.dot(
         attended.reshape(-1, channels), w_out, preferred_element_type=jnp.float32

time: 113 us -> 102 us (0.903)
  blocking collectives: 42.7 us -> 18.2 us
  other arithmetic: 19 us -> 4.82 us
  starting transfers between devices: 7.72 us -> 17.8 us
  waiting for transfers between devices: 6.9 us -> 16.4 us
  matrix products: 20.3 us -> 25.8 us
  local copies, waits for them, and re-layouts: 15.9 us -> 18.5 us
    all_to_all x1 -> x0, blocking collectives: 24.7 us -> none  [per_device(): lax.all_to_all(normed, 'ta', split_axis=2, concat_axis=0, tiled=True)]
    sub x1, other arithmetic: 17.7 us -> 3.42 us  [attend(): expo = jnp.exp(scores - peak)]
    ppermute x0 -> x3, waiting for transfers between devices: none -> 10.2 us  [try_all_the_sizes(): lax.ppermute(aux, lane_axis, [(kk, (kk + hop_no) % opened) for kk in rang...]
    ppermute x0 -> x3, starting transfers between devices: none -> 10.1 us  [try_all_the_sizes(): lax.ppermute(aux, lane_axis, [(kk, (kk + hop_no) % opened) for kk in rang...]
    dot_general x1, matrix products: 1.72 us -> 4.44 us  [attend(): jnp.einsum('rwhfg,grwhd->frwhd', probs, valueset.reshape(shape), preferre...]
    gather x0 -> x1, local copies, waits for them, and re-layouts: none -> 1.6 us  [try_all_the_sizes(): reply = jnp.stack(windows)[(answer - jnp.arange(opened)) % opened]]
    dot_general x3, matrix products: 2.4 us -> 3.93 us  [temporal_mix(): jnp.dot(window.reshape(-1, channels), w_time[tap_index], preferred_elemen...]
    unnamed x16 -> x24, local copies, waits for them, and re-layouts: 0.04 us -> 1.55 us
  transfers between devices with their start and end apart: 3 -> 6, of which waited for: 3 -> 4; matrix products, arithmetic and copies ran while one was open for 3% -> 4% of each run, Pallas kernels for 0% -> 0%
where the time goes in v1:
time: 102 us
  matrix products  25.8 us (25%)
  local copies, waits for them, and re-layouts  18.5 us (18%)
  blocking collectives  18.2 us (18%)
  starting transfers between devices  17.8 us (17%)
  waiting for transfers between devices  16.4 us (16%)
  other arithmetic  4.82 us (5%)
    all_to_all x1, blocking collectives, attend_back(): return lax.all_to_all(output, 'ta', split_axis=0, concat_axis=2, tiled=True)  18.2 us
    ppermute x3, waiting for transfers between devices, try_all_the_sizes(): lax.ppermute(aux, lane_axis, [(kk, (kk + hop_no) % opened) for kk in rang...  10.2 us
    ppermute x3, starting transfers between devices, try_all_the_sizes(): lax.ppermute(aux, lane_axis, [(kk, (kk + hop_no) % opened) for kk in rang...  10.1 us
    dot_general x9, matrix products, conv_space(): jnp.dot(window.reshape(-1, channels), w_space[row_off, col_off], preferre...  8.59 us
    ppermute x1, starting transfers between devices, padded_2(): lax.ppermute(lax.slice_in_dim(block, block.shape[dim] - width, None, axis...  4.97 us
    dot_general x1, matrix products, attend(): jnp.einsum('rwhfg,grwhd->frwhd', probs, valueset.reshape(shape), preferre...  4.44 us
    ppermute x1, waiting for transfers between devices, padded_2(): lax.ppermute(lax.slice_in_dim(block, 0, width, axis=dim), axis, backward)  4.27 us
    dot_general x1, matrix products, attend(): jnp.einsum('frwhd,grwhd->rwhfg', queries.reshape(shape), keyset.reshape(s...  4.11 us
  transfers between devices with their start and end apart: 6, of which 4 were waited for; matrix products, arithmetic and copies ran while one was open for 4% of the time, Pallas kernels for 0%

profile of v1, /device:TPU:0, one launch (start us, length us, event | category | flops | bytes accessed | tf_op | source)
XLA Modules:
  0.0 101.8 jit_solution(7040172855501218752)
XLA Ops:
  0.0 1.2 %fusion.81 = (bf16[4,1,64,512]{3,2,1,0:T(8,128)(2,1)S(1)}, bf16[4,1,64,512]{3,2,1,0:T(8,128)(2,1)S(1)}) fusion(bf16[4,4,64,512]{3,2,1,0:T(8,128)(2,1)} %param.6), kind=kLoop, calls=%fused_computation.100 | loop fusion | bytes 1048576 | tf_op jit(solution)/shard_map/slice | solution.py:43
  1.2 5.0 %collective-permute-start = (bf16[4,1,64,512]{3,2,1,0:T(8,128)(2,1)S(1)}, bf16[4,1,64,512]{3,2,1,0:T(8,128)(2,1)S(1)}, u32[]{:S(2)}, u32[]{:S(2)}) collective-permute-start(bf16[4,1,64,512]{3,2,1,0:T(8,128)(2,1)S(1)} %get-tuple-element.12), channel_id=1, source_target_pairs={{0,1},{1,2},{2,3},{4,5},{5,6},{6,7},{8,9},{9,10},{10,11},{12,13},{... | collective-permute-start | bytes 786440 | tf_op jit(solution)/shard_map/ppermute | solution.py:42
  6.2 0.0 copy-start.2
  6.2 1.4 %collective-permute-start.1 = (bf16[4,1,64,512]{3,2,1,0:T(8,128)(2,1)S(1)}, bf16[4,1,64,512]{3,2,1,0:T(8,128)(2,1)S(1)}, u32[]{:S(2)}, u32[]{:S(2)}) collective-permute-start(bf16[4,1,64,512]{3,2,1,0:T(8,128)(2,1)S(1)} %get-tuple-element.13), channel_id=1, source_target_pairs={{1,0},{2,1},{3,2},{5,4},{6,5},{7,6},{9,8},{10,9},{11,10},{13,12},{... | collective-permute-start | bytes 786440 | tf_op jit(solution)/shard_map/ppermute | solution.py:45
  7.6 2.2 %fusion.55 = f32[4,4,64,512]{3,2,1,0:T(8,128)S(1)} fusion(bf16[4,4,64,512]{3,2,1,0:T(8,128)(2,1)} %param.6, bf16[3,3,512,512]{3,2,1,0:T(8,128)(2,1)} %param.7), kind=kOutput, calls=%fused_computation.64 | convolution fusion | flops 536870912 | bytes 3670016 | tf_op jit(solution)/shard_map/dot_general | solution.py:62
  9.8 1.9 %collective-permute-done = bf16[4,1,64,512]{3,2,1,0:T(8,128)(2,1)S(1)} collective-permute-done((bf16[4,1,64,512]{3,2,1,0:T(8,128)(2,1)S(1)}, bf16[4,1,64,512]{3,2,1,0:T(8,128)(2,1)S(1)}, u32[]{:S(2)}, u32[]{:S(2)}) %collective-permute-start) | collective-permute-done | bytes 262176 | tf_op jit(solution)/shard_map/ppermute | solution.py:42
  11.7 4.3 %collective-permute-done.1 = bf16[4,1,64,512]{3,2,1,0:T(8,128)(2,1)S(1)} collective-permute-done((bf16[4,1,64,512]{3,2,1,0:T(8,128)(2,1)S(1)}, bf16[4,1,64,512]{3,2,1,0:T(8,128)(2,1)S(1)}, u32[]{:S(2)}, u32[]{:S(2)}) %collective-permute-start.1) | collective-permute-done | bytes 262176 | tf_op jit(solution)/shard_map/ppermute | solution.py:45
  16.0 0.9 fusion.22
  16.9 0.7 fusion.35
  17.6 0.7 fusion.37
  18.3 0.7 fusion.39
  19.0 0.7 fusion.41
  19.8 0.7 fusion.43
  20.5 0.7 fusion.23
  21.2 0.7 fusion.27
  21.9 1.4 %multiply_convert_fusion = bf16[4,4,64,512]{3,2,1,0:T(8,128)(2,1)S(1)} fusion(f32[4,4,64,512]{3,2,1,0:T(8,128)S(1)} %fusion.27, f32[4,4,64,512]{3,2,1,0:T(8,128)S(1)} %fusion.35, f32[4,4,64,512]{3,2,1,0:T(8,128)S(1)} %fusion.37, f32[4,4,64,512]{3,2,1,0:T(8,128)S(1)} %fusion.55, f32[4,4,64,512]{3,2,1,0:T(8,128)S(1)} %fusion.39, ...), kind=kOutput, calls=%fused_computation.26 | convolution fusion | flops 543686656 | bytes 19398656 | tf_op jit(solution)/shard_map/dot_general | solution.py:62
  23.3 0.0 copy-start.3
  23.4 1.0 copy-done.3
  24.3 0.8 slice.126
  25.2 1.3 %collective-permute-start.2 = (bf16[2,4,64,512]{3,2,1,0:T(8,128)(2,1)}, bf16[2,4,64,512]{3,2,1,0:T(8,128)(2,1)S(1)}, u32[]{:S(2)}, u32[]{:S(2)}) collective-permute-start(bf16[2,4,64,512]{3,2,1,0:T(8,128)(2,1)} %slice.126), channel_id=1, source_target_pairs={{0,4},{4,8},{8,12},{1,5},{5,9},{9,13},{2,6},{6,10},{10,14},{3,7},{... | collective-permute-start | bytes 1572872 | tf_op jit(solution)/shard_map/ppermute | solution.py:53
  26.5 0.0 copy-start.9
  26.5 2.2 %fusion.49 = f32[4,4,64,512]{3,2,1,0:T(8,128)S(1)} fusion(bf16[4,4,64,512]{3,2,1,0:T(8,128)(2,1)} %copy-done.3, bf16[3,512,512]{2,1,0:T(8,128)(2,1)} %param.8), kind=kOutput, calls=%fused_computation.58 | convolution fusion | flops 536870912 | bytes 3670016 | tf_op jit(solution)/shard_map/dot_general | solution.py:78
  28.8 0.7 fusion.45
  29.5 1.0 %fusion.5 = (f32[4,4,64]{2,1,0:T(4,128)S(1)}, bf16[4,4,64,512]{3,2,1,0:T(8,128)(2,1)S(1)}) fusion(bf16[3,512,512]{2,1,0:T(8,128)(2,1)S(1)} %copy-done.9, bf16[4,4,64,512]{3,2,1,0:T(8,128)(2,1)S(1)} %copy-done.4, bf16[2,4,64,512]{3,2,1,0:T(8,128)(2,1)S(1)} %collective-permute-done.2, f32[4,4,64,512]{3,2,1,0:T(8,128)S(1)} %fusion.49, ...), kind=kOutput, calls=%fused_computation.13 | convolution fusion | flops 544209920 | bytes 8392704 | tf_op jit(solution)/shard_map/dot_general | solution.py:78
  30.5 0.0 copy-start.5
  30.6 0.3 fusion.7
  30.9 0.1 dynamic-slice_bitcast_fusion.3
  31.0 0.5 copy-done.5
  31.5 6.3 %collective-permute-start.3 = (bf16[4,4,16,512]{3,2,1,0:T(8,128)(2,1)S(1)}, bf16[4,4,16,512]{3,2,1,0:T(8,128)(2,1)S(1)}, u32[]{:S(2)}, u32[]{:S(2)}) collective-permute-start(bf16[4,4,16,512]{3,2,1,0:T(8,128)(2,1)S(1)} %get-tuple-element.11), channel_id=1, source_target_pairs={{0,4},{4,8},{8,12},{12,0},{1,5},{5,9},{9,13},{13,1},{2,6},{6,10},{... | collective-permute-start | bytes 786440 | tf_op jit(solution)/shard_map/ppermute | solution.py:28
  37.8 2.3 %collective-permute-start.4 = (bf16[4,4,16,512]{3,2,1,0:T(8,128)(2,1)S(1)}, bf16[4,4,16,512]{3,2,1,0:T(8,128)(2,1)S(1)}, u32[]{:S(2)}, u32[]{:S(2)}) collective-permute-start(bf16[4,4,16,512]{3,2,1,0:T(8,128)(2,1)S(1)} %get-tuple-element.10), channel_id=1, source_target_pairs={{0,8},{4,12},{8,0},{12,4},{1,9},{5,13},{9,1},{13,5},{2,10},{6,14},... | collective-permute-start | bytes 786440 | tf_op jit(solution)/shard_map/ppermute | solution.py:28
  40.1 1.5 %collective-permute-start.5 = (bf16[4,4,16,512]{3,2,1,0:T(8,128)(2,1)S(1)}, bf16[4,4,16,512]{3,2,1,0:T(8,128)(2,1)S(1)}, u32[]{:S(2)}, u32[]{:S(2)}) collective-permute-start(bf16[4,4,16,512]{3,2,1,0:T(8,128)(2,1)S(1)} %get-tuple-element.9), channel_id=1, source_target_pairs={{0,12},{4,0},{8,4},{12,8},{1,13},{5,1},{9,5},{13,9},{2,14},{6,2},{... | collective-permute-start | bytes 786440 | tf_op jit(solution)/shard_map/ppermute | solution.py:28
  41.6 5.2 %collective-permute-done.4 = bf16[4,4,16,512]{3,2,1,0:T(8,128)(2,1)S(1)} collective-permute-done((bf16[4,4,16,512]{3,2,1,0:T(8,128)(2,1)S(1)}, bf16[4,4,16,512]{3,2,1,0:T(8,128)(2,1)S(1)}, u32[]{:S(2)}, u32[]{:S(2)}) %collective-permute-start.4) | collective-permute-done | bytes 262176 | tf_op jit(solution)/shard_map/ppermute | solution.py:28
  46.8 5.0 %collective-permute-done.5 = bf16[4,4,16,512]{3,2,1,0:T(8,128)(2,1)S(1)} collective-permute-done((bf16[4,4,16,512]{3,2,1,0:T(8,128)(2,1)S(1)}, bf16[4,4,16,512]{3,2,1,0:T(8,128)(2,1)S(1)}, u32[]{:S(2)}, u32[]{:S(2)}) %collective-permute-start.5) | collective-permute-done | bytes 262176 | tf_op jit(solution)/shard_map/ppermute | solution.py:28
  51.8 0.1 pad_maximum_fusion.1
  52.0 1.6 %gather_fusion = bf16[4,4,4,16,512]{4,3,2,1,0:T(8,128)(2,1)} fusion(bf16[4,4,4,16,512]{4,3,2,1,0:T(8,128)(2,1)S(1)} %pad_maximum_fusion.1, s32[1024]{0:T(1024)S(1)} %pad_clamp_fusion), kind=kCustom, calls=%fused_computation | custom fusion | bytes 2097168 | tf_op jit(solution)/shard_map/gather | solution.py:30
  53.6 3.0 %convolution_convert_fusion = bf16[1024,1536]{1,0:T(8,128)(2,1)S(1)} fusion(bf16[1024,512]{1,0:T(8,128)(2,1)} %bitcast.129, bf16[512,1536]{1,0:T(8,128)(2,1)S(1)} %copy-done), kind=kOutput, calls=%fused_computation.6 | convolution fusion | flops 1612185600 | bytes 5767168 | tf_op jit(solution)/shard_map/dot_general | solution.py:91
  56.6 1.8 %fusion.80 = (bf16[16,4,16,512]{3,2,1,0:T(8,128)(2,1)}, bf16[16,4,16,512]{3,2,1,0:T(8,128)(2,1)}, bf16[16,4,16,512]{3,2,1,0:T(8,128)(2,1)}) fusion(bf16[16,4,16,1536]{3,2,1,0:T(8,128)(2,1)S(1)} %bitcast.128), kind=kLoop, calls=%fused_computation.99 | loop fusion | bytes 6291456 | tf_op jit(solution)/shard_map/slice | solution.py:98
  58.3 2.8 %reshape.140 = bf16[16,4,16,8,64]{4,3,2,1,0:T(8,128)(2,1)S(1)} reshape(bf16[16,4,16,512]{3,2,1,0:T(8,128)(2,1)} %get-tuple-element.7) | data formatting | bytes 2097152 | tf_op jit(solution)/shard_map/reshape | solution.py:108
  61.1 3.9 %reshape.141 = bf16[16,4,16,8,64]{4,3,2,1,0:T(8,128)(2,1)} reshape(bf16[16,4,16,512]{3,2,1,0:T(8,128)(2,1)} %get-tuple-element.6) | data formatting | bytes 2097152 | tf_op jit(solution)/shard_map/reshape | solution.py:109
  65.0 4.1 %fusion.11 = f32[4,16,8,16,16]{3,4,2,1,0:T(8,128)S(1)} fusion(bf16[16,4,16,8,64]{4,3,2,1,0:T(8,128)(2,1)} %reshape.141, bf16[16,4,16,8,64]{4,3,2,1,0:T(8,128)(2,1)S(1)} %reshape.140), kind=kOutput, calls=%fused_computation.19 | convolution fusion | flops 16777216 | bytes 2621440 | tf_op jit(solution)/shard_map/frwhd,grwhd->rwhfg/dot_general | solution.py:106
  69.1 3.4 %fusion.82 = (f32[4,16,8,16]{3,2,1,0:T(8,128)S(1)}, f32[4,16,8,16,16]{3,4,2,1,0:T(8,128)}) fusion(f32[4,16,8,16,16]{3,4,2,1,0:T(8,128)S(1)} %fusion.11), kind=kOutput, calls=%fused_computation.101 | output fusion | flops 524303 | bytes 1081344 | tf_op jit(solution)/shard_map/sub | solution.py:114
  72.6 2.1 %reshape.139 = bf16[16,4,16,8,64]{4,3,2,1,0:T(8,128)(2,1)} reshape(bf16[16,4,16,512]{3,2,1,0:T(8,128)(2,1)S(1)} %copy-done.7) | data formatting | bytes 2097152 | tf_op jit(solution)/shard_map/reshape | solution.py:117
  74.7 4.4 %convert_bitcast_fusion = bf16[16,4,16,8,64]{4,0,3,2,1:T(8,128)(2,1)S(1)} fusion(f32[4,16,8,16,16]{3,4,2,1,0:T(8,128)} %get-tuple-element.17, f32[4,16,8,16]{3,2,1,0:T(8,128)S(1)} %get-tuple-element.16, bf16[16,4,16,8,64]{4,3,2,1,0:T(8,128)(2,1)} %reshape.139), kind=kOutput, calls=%fused_computation.22 | convolution fusion | flops 17563648 | bytes 2654208 | tf_op jit(solution)/shard_map/rwhfg,grwhd->frwhd/dot_general | solution.py:116
  79.1 0.5 copy.12
  79.7 2.1 %convert_element_type.45 = bf16[16,4,16,512]{3,2,1,0:T(8,128)(2,1)} reshape(bf16[16,4,16,8,64]{4,3,2,1,0:T(8,128)(2,1)S(1)} %copy.12) | data formatting | bytes 2097152 | tf_op jit(solution)/shard_map/convert_element_type | solution.py:119
  81.7 18.2 %all_to_all.15 = bf16[16,4,16,512]{3,2,1,0:T(8,128)(2,1)S(1)} all-to-all(bf16[16,4,16,512]{3,2,1,0:T(8,128)(2,1)} %convert_element_type.45), channel_id=1, replica_groups=mesh['ga'=2,'ta'=4,'gy'=4] {'ta'}, dimensions={0} | all-to-all | bytes 2097152 | tf_op jit(solution)/shard_map/all_to_all | solution.py:124
  99.9 0.1 copy.13
  100.1 1.7 %fusion.8 = bf16[4,4,64,512]{3,2,1,0:T(8,128)(2,1)} fusion(bf16[4,4,64,512]{3,2,1,0:T(8,128)(2,1)S(1)} %copy-done.6, bf16[4,4,64,512]{3,2,1,0:T(8,128)(2,1)S(1)} %bitcast.130, bf16[512,512]{1,0:T(8,128)(2,1)S(1)} %copy-done.11), kind=kOutput, calls=%fused_computation.16 | convolution fusion | flops 538443776 | bytes 3670016 | tf_op jit(solution)/shard_map/dot_general | solution.py:136
  (23 shorter events, 0.1 us)
Async XLA Ops:
  0.0 53.6 %copy-start = (bf16[512,1536]{1,0:T(8,128)(2,1)S(1)}, bf16[512,1536]{1,0:T(8,128)(2,1)}, u32[]{:S(2)}) copy-start(bf16[512,1536]{1,0:T(8,128)(2,1)} %param.9) | copy-start | bytes 4718596
  1.2 10.5 %collective-permute-start = (bf16[4,1,64,512]{3,2,1,0:T(8,128)(2,1)S(1)}, bf16[4,1,64,512]{3,2,1,0:T(8,128)(2,1)S(1)}, u32[]{:S(2)}, u32[]{:S(2)}) collective-permute-start(bf16[4,1,64,512]{3,2,1,0:T(8,128)(2,1)S(1)} %get-tuple-element.12), channel_id=1, source_target_pairs={{0,1},{1,2},{2,3},{4,5},{5,6},{6,7},{8,9},{9,10},{10,11},{12,13},{... | collective-permute-start | bytes 786440 | tf_op jit(solution)/shard_map/ppermute | solution.py:42
  6.2 9.8 %copy-start.2 = (bf16[4,4,64,512]{3,2,1,0:T(8,128)(2,1)S(1)}, bf16[4,4,64,512]{3,2,1,0:T(8,128)(2,1)}, u32[]{:S(2)}) copy-start(bf16[4,4,64,512]{3,2,1,0:T(8,128)(2,1)} %param.6) | copy-start | bytes 3145732
  6.2 9.8 %collective-permute-start.1 = (bf16[4,1,64,512]{3,2,1,0:T(8,128)(2,1)S(1)}, bf16[4,1,64,512]{3,2,1,0:T(8,128)(2,1)S(1)}, u32[]{:S(2)}, u32[]{:S(2)}) collective-permute-start(bf16[4,1,64,512]{3,2,1,0:T(8,128)(2,1)S(1)} %get-tuple-element.13), channel_id=1, source_target_pairs={{1,0},{2,1},{3,2},{5,4},{6,5},{7,6},{9,8},{10,9},{11,10},{13,12},{... | collective-permute-start | bytes 786440 | tf_op jit(solution)/shard_map/ppermute | solution.py:45
  7.6 9.3 %copy-start.8 = (bf16[3,3,512,512]{3,2,1,0:T(8,128)(2,1)S(1)}, bf16[3,3,512,512]{3,2,1,0:T(8,128)(2,1)}, u32[]{:S(2)}) copy-start(bf16[3,3,512,512]{3,2,1,0:T(8,128)(2,1)} %param.7) | copy-start | bytes 14155780
  23.3 1.0 copy-start.3
  25.2 3.6 %collective-permute-start.2 = (bf16[2,4,64,512]{3,2,1,0:T(8,128)(2,1)}, bf16[2,4,64,512]{3,2,1,0:T(8,128)(2,1)S(1)}, u32[]{:S(2)}, u32[]{:S(2)}) collective-permute-start(bf16[2,4,64,512]{3,2,1,0:T(8,128)(2,1)} %slice.126), channel_id=1, source_target_pairs={{0,4},{4,8},{8,12},{1,5},{5,9},{9,13},{2,6},{6,10},{10,14},{3,7},{... | collective-permute-start | bytes 1572872 | tf_op jit(solution)/shard_map/ppermute | solution.py:53
  26.5 2.2 %copy-start.4 = (bf16[4,4,64,512]{3,2,1,0:T(8,128)(2,1)S(1)}, bf16[4,4,64,512]{3,2,1,0:T(8,128)(2,1)}, u32[]{:S(2)}) copy-start(bf16[4,4,64,512]{3,2,1,0:T(8,128)(2,1)} %copy-done.3) | copy-start | bytes 3145732
  26.5 2.2 %copy-start.9 = (bf16[3,512,512]{2,1,0:T(8,128)(2,1)S(1)}, bf16[3,512,512]{2,1,0:T(8,128)(2,1)}, u32[]{:S(2)}) copy-start(bf16[3,512,512]{2,1,0:T(8,128)(2,1)} %param.8) | copy-start | bytes 4718596
  29.5 1.1 %copy-start.10 = (f32[512]{0:T(512)S(1)}, f32[512]{0:T(512)}, u32[]{:S(2)}) copy-start(f32[512]{0:T(512)} %param.11) | copy-start | bytes 6148
  30.5 1.0 copy-start.5
  31.5 10.1 %collective-permute-start.3 = (bf16[4,4,16,512]{3,2,1,0:T(8,128)(2,1)S(1)}, bf16[4,4,16,512]{3,2,1,0:T(8,128)(2,1)S(1)}, u32[]{:S(2)}, u32[]{:S(2)}) collective-permute-start(bf16[4,4,16,512]{3,2,1,0:T(8,128)(2,1)S(1)} %get-tuple-element.11), channel_id=1, source_target_pairs={{0,4},{4,8},{8,12},{12,0},{1,5},{5,9},{9,13},{13,1},{2,6},{6,10},{... | collective-permute-start | bytes 786440 | tf_op jit(solution)/shard_map/ppermute | solution.py:28
  37.8 9.0 %collective-permute-start.4 = (bf16[4,4,16,512]{3,2,1,0:T(8,128)(2,1)S(1)}, bf16[4,4,16,512]{3,2,1,0:T(8,128)(2,1)S(1)}, u32[]{:S(2)}, u32[]{:S(2)}) collective-permute-start(bf16[4,4,16,512]{3,2,1,0:T(8,128)(2,1)S(1)} %get-tuple-element.10), channel_id=1, source_target_pairs={{0,8},{4,12},{8,0},{12,4},{1,9},{5,13},{9,1},{13,5},{2,10},{6,14},... | collective-permute-start | bytes 786440 | tf_op jit(solution)/shard_map/ppermute | solution.py:28
  40.1 11.7 %collective-permute-start.5 = (bf16[4,4,16,512]{3,2,1,0:T(8,128)(2,1)S(1)}, bf16[4,4,16,512]{3,2,1,0:T(8,128)(2,1)S(1)}, u32[]{:S(2)}, u32[]{:S(2)}) collective-permute-start(bf16[4,4,16,512]{3,2,1,0:T(8,128)(2,1)S(1)} %get-tuple-element.9), channel_id=1, source_target_pairs={{0,12},{4,0},{8,4},{12,8},{1,13},{5,1},{9,5},{13,9},{2,14},{6,2},{... | collective-permute-start | bytes 786440 | tf_op jit(solution)/shard_map/ppermute | solution.py:28
  69.1 3.4 %copy-start.7 = (bf16[16,4,16,512]{3,2,1,0:T(8,128)(2,1)S(1)}, bf16[16,4,16,512]{3,2,1,0:T(8,128)(2,1)}, u32[]{:S(2)}) copy-start(bf16[16,4,16,512]{3,2,1,0:T(8,128)(2,1)} %get-tuple-element.5) | copy-start | bytes 3145732
  81.7 18.3 %copy-start.6 = (bf16[4,4,64,512]{3,2,1,0:T(8,128)(2,1)S(1)}, bf16[4,4,64,512]{3,2,1,0:T(8,128)(2,1)}, u32[]{:S(2)}) copy-start(bf16[4,4,64,512]{3,2,1,0:T(8,128)(2,1)} %copy-done.5) | copy-start | bytes 3145732
  81.7 18.3 %copy-start.11 = (bf16[512,512]{1,0:T(8,128)(2,1)S(1)}, bf16[512,512]{1,0:T(8,128)(2,1)}, u32[]{:S(2)}) copy-start(bf16[512,512]{1,0:T(8,128)(2,1)} %param.10) | copy-start | bytes 1572868
  100.0 1.7 %copy-start.1 = (bf16[512,1536]{1,0:T(8,128)(2,1)S(1)}, bf16[512,1536]{1,0:T(8,128)(2,1)}, u32[]{:S(2)}) copy-start(bf16[512,1536]{1,0:T(8,128)(2,1)} %param.9) | copy-start | bytes 4718596
